TPU v7x, 256 devices: a whole 4x4x8 slice. The times are simulated.
256 devices in a mesh: space: 64 (over z, y, core), tm: 4 (over x).
Axes of the slice: x: 4, y: 4, z: 8, core: 2. Of those that a mesh axis runs over, the one named last changes fastest.
Arguments:
- precip: float32 [512, 384, 2048], P('tm', 'space'), may hold values from 0.0001 to 0.01
Outputs:
- totals: float32 [384, 2048, 512], P(None, 'space', 'tm')
All inputs are finite; a program needn't handle non-finite values.
Results may differ from a plain program's by a relative error of at most 0.00005.
Values sent between devices are 32-bit elements; how exact they have to be, the bound alone decides.
No kernel may reach another device: no remote copies, remote signals or barrier semaphores. Data moves between devices by JAX's collectives and lax.ppermute only.
A program may use at most 64 MiB of HBM per device.

v0:
```python
import functools

import jax
import jax.numpy as jnp
from jax import lax
from jax.experimental import pallas as pl
from jax.experimental.pallas import tpu as pltpu
from jax.sharding import Mesh
from jax.sharding import PartitionSpec as P

PLANE = ("space_1", "space_2")
RING_FIRST = (4, 3, -3)
PLANE_FIRST = (0, 1, -1, 2, -2)
PARTS = 3
PIECES = 4

IN_VMEM = pl.BlockSpec(memory_space=pltpu.VMEM)
IN_HBM = pl.BlockSpec(memory_space=pl.ANY)
LIMIT = pltpu.CompilerParams(vmem_limit_bytes=12 * 2**20)
JOIN = pltpu.CompilerParams(vmem_limit_bytes=65_300_000)
WIDE = pltpu.CompilerParams(vmem_limit_bytes=64_800_000)


def hbm(shape):
    return pltpu.HBM(shape, jnp.float32)


def ring_place(step, ring):
    return lax.rem(lax.axis_index("space_0") + (step + ring), ring)


def carried(theirs_ref, blocks_before, row, lanes):
    carry = None
    for q in range(theirs_ref.shape[0]):
        line = jnp.where(q < blocks_before, theirs_ref[q, pl.ds(row, 1), lanes], 0.0)
        carry = line if carry is None else carry + line
    return carry


def running_kernel(sources, carry_of, out_ref, days_buf, parts_buf, out_buf, in_sems, out_sems):
    n = len(sources)
    rows, days, width = days_buf.shape[1:]
    plane, cell = out_buf.shape[1], out_buf.shape[3]
    reads = [pltpu.make_async_copy(sources[k], days_buf.at[k], in_sems.at[k]) for k in range(n)]
    writes = [
        pltpu.make_async_copy(out_buf.at[k], out_ref.at[:, k], out_sems.at[k]) for k in range(n)
    ]
    for copy in reads:
        copy.start()
    earlier = lax.broadcasted_iota(jnp.int32, (days, days), 0)
    later = lax.broadcasted_iota(jnp.int32, (days, days), 1)
    upto = (earlier <= later).astype(jnp.bfloat16)
    upto = jnp.concatenate([upto] * PARTS, 0)
    first = lax.broadcasted_iota(jnp.int32, (days, width), 0) == 0
    for k in range(n):
        reads[k].wait()
        for r in range(rows):
            x = days_buf[k, r]
            x = jnp.where(first, x + carry_of(k, r), x).T
            for p in range(PARTS):
                part = x.astype(jnp.bfloat16)
                parts_buf[k % 2, r, :, pl.ds(p * days, days)] = part
                x = x - part.astype(jnp.float32)
        for r in range(rows):
            total = jnp.dot(parts_buf[k % 2, r], upto, preferred_element_type=jnp.float32)
            out_buf[k, :, r] = total.reshape(plane, cell, days)
        writes[k].start()
    for copy in writes:
        copy.wait()


def column_kernel(days_ref, theirs_ref, out_ref, *scratch, steps, ring):
    width = days_ref.shape[2] // ring
    lanes = [
        pl.ds(pl.multiple_of(ring_place(s, ring) * width, width), width) for s in steps
    ]
    running_kernel(
        [days_ref.at[:, :, part] for part in lanes],
        lambda k, r: carried(theirs_ref, lax.axis_index("tm"), r, lanes[k]),
        out_ref,
        *scratch,
    )


def cut_kernel(days_ref, *refs, steps, ring):
    n = len(steps)
    out_refs, buf, in_sems, out_sems = refs[:n], refs[n], refs[n + 1], refs[n + 2]
    width = days_ref.shape[2] // ring
    reads, writes = [], []
    for k, step in enumerate(steps):
        lanes = pl.ds(pl.multiple_of(ring_place(step, ring) * width, width), width)
        reads.append(pltpu.make_async_copy(days_ref.at[:, :, lanes], buf.at[k], in_sems.at[k]))
        writes.append(pltpu.make_async_copy(buf.at[k], out_refs[k], out_sems.at[k]))
    for copy in reads:
        copy.start()
    for read, write in zip(reads, writes):
        read.wait()
        write.start()
    for copy in writes:
        copy.wait()


def cut_columns(by_row, ring, steps):
    rows, days, lon = by_row.shape
    n = len(steps)
    shape = (rows, days, lon // ring)
    return pl.pallas_call(
        functools.partial(cut_kernel, steps=steps, ring=ring),
        compiler_params=LIMIT,
        in_specs=[IN_HBM],
        out_specs=[IN_HBM] * n,
        out_shape=[hbm(shape)] * n,
        scratch_shapes=[
            pltpu.VMEM((n, *shape), jnp.float32),
            pltpu.SemaphoreType.DMA((n,)),
            pltpu.SemaphoreType.DMA((n,)),
        ],
    )(by_row)


def lead_kernel(days_ref, out_ref, sem, *, step, ring):
    width = days_ref.shape[2] // ring
    lanes = pl.ds(pl.multiple_of(ring_place(step, ring) * width, width), width)
    copy = pltpu.make_async_copy(days_ref.at[:, :, lanes], out_ref, sem)
    copy.start()
    copy.wait()


def lead_column(by_row, ring, step):
    rows, days, lon = by_row.shape
    return pl.pallas_call(
        functools.partial(lead_kernel, step=step, ring=ring),
        compiler_params=LIMIT,
        in_specs=[IN_HBM],
        out_specs=IN_VMEM,
        out_shape=pltpu.VMEM((rows, days, lon // ring), jnp.float32),
        scratch_shapes=[pltpu.SemaphoreType.DMA],
    )(by_row)


def block_kernel(*refs, n):
    blocks, lines, rest = refs[:n], refs[n : 2 * n], refs[2 * n :]
    out_ref, *scratch = rest[-6:]
    running_kernel(blocks, lambda k, r: lines[k][pl.ds(r, 1)], out_ref, *scratch)


def running_call(body, specs, args, n, rows, days, width, plane, params=LIMIT):
    cell = width // plane
    return pl.pallas_call(
        body,
        compiler_params=params,
        in_specs=specs,
        out_specs=IN_HBM,
        out_shape=hbm((plane, n, rows, cell, days)),
        scratch_shapes=[
            pltpu.VMEM((n, rows, days, width), jnp.float32),
            pltpu.VMEM((2, rows, width, PARTS * days), jnp.bfloat16),
            pltpu.VMEM((n, plane, rows, cell, days), jnp.float32),
            pltpu.SemaphoreType.DMA((n,)),
            pltpu.SemaphoreType.DMA((n,)),
        ],
    )(*args)


def running_columns(by_row, theirs, ring, steps, plane):
    rows, days, lon = by_row.shape
    body = functools.partial(column_kernel, steps=steps, ring=ring)
    specs = [IN_HBM, IN_VMEM]
    args = (by_row, theirs)
    return running_call(body, specs, args, len(steps), rows, days, lon // ring, plane)


def running_blocks(blocks, lines, plane):
    n = len(blocks)
    body = functools.partial(block_kernel, n=n)
    specs = [IN_HBM] * n + [IN_VMEM] * n
    return running_call(body, specs, (*blocks, *lines), n, *blocks[0].shape, plane, JOIN)


def totals_kernel(days_ref, total_ref, days_buf, sems):
    rows, _, lon = days_ref.shape
    cuts = sems.shape[0]
    width = lon // cuts
    copies = [
        pltpu.make_async_copy(
            days_ref.at[:, :, pl.ds(c * width, width)], days_buf.at[:, :, pl.ds(c * width, width)], sems.at[c]
        )
        for c in range(cuts)
    ]
    for copy in copies:
        copy.start()
    for c in range(cuts):
        copies[c].wait()
        for r in range(rows):
            line = jnp.sum(days_buf[r, :, pl.ds(c * width, width)], axis=0, keepdims=True)
            for q in range(total_ref.shape[0]):
                total_ref[q, pl.ds(r, 1), pl.ds(c * width, width)] = line


def block_totals(by_row, copies, cuts=8):
    rows, _, lon = by_row.shape
    return pl.pallas_call(
        totals_kernel,
        compiler_params=LIMIT,
        in_specs=[IN_HBM],
        out_specs=IN_VMEM,
        out_shape=jax.ShapeDtypeStruct((copies, rows, lon), jnp.float32),
        scratch_shapes=[pltpu.VMEM(by_row.shape, jnp.float32), pltpu.SemaphoreType.DMA((cuts,))],
    )(by_row)


def lines_kernel(theirs_ref, *line_refs, steps, ring):
    width = theirs_ref.shape[2] // ring
    for step, line_ref in zip(steps, line_refs):
        lanes = pl.ds(pl.multiple_of(ring_place(step, ring) * width, width), width)
        line_ref[...] = jnp.zeros_like(line_ref)
        for r in range(theirs_ref.shape[1]):
            line_ref[pl.ds(r, 1)] = carried(theirs_ref, lax.axis_index("tm"), r, lanes)


def carry_lines(theirs, steps, ring):
    width = theirs.shape[2] // ring
    return pl.pallas_call(
        functools.partial(lines_kernel, steps=steps, ring=ring),
        compiler_params=LIMIT,
        in_specs=[IN_VMEM],
        out_specs=[IN_VMEM] * len(steps),
        out_shape=[jax.ShapeDtypeStruct((8, width), jnp.float32)] * len(steps),
    )(theirs)


def place_kernel(piece_ref, *refs, steps):
    whole_ref, buf, in_sems, out_sems = refs[-4:]
    ring = whole_ref.shape[0]
    reads, writes = [], []
    for k, step in enumerate(steps):
        target = whole_ref.at[ring_place(-step, ring)]
        reads.append(pltpu.make_async_copy(piece_ref.at[:, k], buf.at[k], in_sems.at[k]))
        writes.append(pltpu.make_async_copy(buf.at[k], target, out_sems.at[k]))
    for copy in reads:
        copy.start()
    for read, write in zip(reads, writes):
        read.wait()
        write.start()
    for copy in writes:
        copy.wait()


def place(whole, ring, piece, steps):
    plane, _, *block = piece.shape
    n = len(steps)
    args = (piece,) if whole is None else (piece, whole)
    return pl.pallas_call(
        functools.partial(place_kernel, steps=steps),
        compiler_params=WIDE,
        in_specs=[IN_HBM] * len(args),
        out_specs=IN_HBM,
        out_shape=jax.ShapeDtypeStruct((ring, plane, *block), jnp.float32),
        scratch_shapes=[
            pltpu.VMEM((n, plane, *block), jnp.float32),
            pltpu.SemaphoreType.DMA((n,)),
            pltpu.SemaphoreType.DMA((n,)),
        ],
        input_output_aliases={} if whole is None else {1: 0},
    )(*args)


def place_pair_kernel(*refs, steps):
    n = len(steps)
    block_refs, whole_ref, sems = refs[:n], refs[n + 1], refs[n + 2]
    ring = whole_ref.shape[0]
    part = block_refs[0].shape[0] // PIECES
    copies = []
    for k, step in enumerate(steps):
        for p in range(PIECES):
            source = block_refs[k].at[pl.ds(p * part, part)]
            target = whole_ref.at[ring_place(-step, ring), pl.ds(p * part, part)]
            copies.append(pltpu.make_async_copy(source, target, sems.at[k, p]))
    for copy in copies:
        copy.start()
    for copy in copies:
        copy.wait()


def place_blocks(whole, blocks, steps, near):
    n = len(steps)
    if near:
        blocks = [pltpu.with_memory_space_constraint(block, pltpu.VMEM) for block in blocks]
    return pl.pallas_call(
        functools.partial(place_pair_kernel, steps=steps),
        compiler_params=LIMIT if near else WIDE,
        in_specs=[IN_VMEM] * n + [IN_HBM],
        out_specs=IN_HBM,
        out_shape=jax.ShapeDtypeStruct(whole.shape, jnp.float32),
        scratch_shapes=[pltpu.SemaphoreType.DMA((n, PIECES))],
        input_output_aliases={n: 0},
    )(*blocks, whole)


def shifted(block, ring, step):
    return lax.ppermute(block, "space_0", [(i, (i + step) % ring) for i in range(ring)])


def exchanged(value, axes):
    return lax.all_to_all(value, axes, split_axis=0, concat_axis=0, tiled=True)


def per_device(precip):
    by_row = jnp.transpose(precip, (1, 0, 2))
    stays = pltpu.with_memory_space_constraint(by_row, pltpu.HBM)
    rows, days, lon = by_row.shape
    ring = lax.axis_size("space_0")
    plane = lax.axis_size("space_1") * lax.axis_size("space_2")
    blocks = lax.axis_size("tm")

    def sent(block, step):
        return shifted(block, ring, step)

    raw = [sent(lead_column(stays, ring, RING_FIRST[0]), RING_FIRST[0])]
    cut = cut_columns(stays, ring, RING_FIRST[1:])
    raw += [sent(cut[k - 1], RING_FIRST[k]) for k in (1, 2)]
    theirs = block_totals(stays, blocks)
    theirs = exchanged(theirs, "tm")
    mixed = running_columns(stays, theirs, ring, PLANE_FIRST, plane)
    mixed = exchanged(mixed, PLANE)
    lines = carry_lines(theirs, RING_FIRST, ring)
    lines = [sent(line, step) for line, step in zip(lines, RING_FIRST)]
    late = [sent(mixed[:, k], PLANE_FIRST[k]) for k in range(1, len(PLANE_FIRST))]
    second = running_blocks(raw, lines, plane)
    second = exchanged(second, PLANE)
    whole = place(None, ring, mixed, (0,))
    whole = place_blocks(whole, late[2:], PLANE_FIRST[3:], False)
    whole = place(whole, ring, second, RING_FIRST)
    whole = place_blocks(whole, late[:2], PLANE_FIRST[1:3], True)
    return whole.reshape(ring * plane * rows, lon // (ring * plane), days)


def solution(mesh):
    finer = Mesh(
        mesh.devices.reshape(8, 4, 2, mesh.shape["tm"]), ("space_0", "space_1", "space_2", "tm")
    )
    space = ("space_0", "space_1", "space_2")
    return jax.shard_map(
        per_device,
        mesh=finer,
        in_specs=(P("tm", space, None),),
        out_specs=P(None, space, "tm"),
        check_vma=False,
    )
```

profile of v0, /device:TPU:10, one launch (start us, length us, event | category | flops | bytes accessed | tf_op | source)
XLA Modules:
  0.0 197.8 jit_solution(68689694694718441)
XLA Ops:
  0.0 3.0 %shard_map.17 = f32[4,6,2048]{2,1,0:T(8,128)S(1)} custom-call(f32[6,128,2048]{2,1,0:T(8,128)} %bitcast.18), custom_call_target="tpu_custom_call" | custom-call | tf_op jit(solution)/shard_map/pallas_call | solution.py:202
  3.0 9.8 %all_to_all.15.theirs_ref = f32[4,6,2048]{2,1,0:T(8,128)S(1)} all-to-all(f32[4,6,2048]{2,1,0:T(8,128)S(1)} %shard_map.17), channel_id=1, replica_groups=mesh['space_0'=8,'space_1'=4,'space_2'=2,'tm'=4] {'tm'}, dimensions={0} | all-to-all | bytes 393216 | tf_op jit(solution)/shard_map/all_to_all | solution.py:305
  12.8 4.9 %shard_map.18 = f32[8,5,6,32,128]{4,3,2,1,0:T(8,128)} custom-call(f32[6,128,2048]{2,1,0:T(8,128)} %bitcast.19, f32[4,6,2048]{2,1,0:T(8,128)S(1)} %all_to_all.15.theirs_ref), custom_call_target="tpu_custom_call" | custom-call | tf_op jit(solution)/shard_map/pallas_call | solution.py:149
  17.7 4.9 %all-to-all-start.1 = ((f32[8,5,6,32,128]{4,3,2,1,0:T(8,128)}), f32[8,5,6,32,128]{4,3,2,1,0:T(8,128)}, u32[]{:S(2)}, u32[]{:S(2)}) async-start(f32[8,5,6,32,128]{4,3,2,1,0:T(8,128)} %shard_map.18), calls=%async_computation.1 | async-start | bytes 7864320 | tf_op jit(solution)/shard_map/all_to_all | solution.py:305
  22.7 2.3 %shard_map.20 = (f32[6,128,256]{2,1,0:T(8,128)}, f32[6,128,256]{2,1,0:T(8,128)}) custom-call(f32[6,128,2048]{2,1,0:T(8,128)} %bitcast.20), custom_call_target="tpu_custom_call" | custom-call | tf_op jit(solution)/shard_map/pallas_call | solution.py:107
  25.0 4.7 %collective-permute-start.3 = (f32[6,128,256]{2,1,0:T(8,128)}, f32[6,128,256]{2,1,0:T(8,128)S(1)}, u32[]{:S(2)}, u32[]{:S(2)}) collective-permute-start(f32[6,128,256]{2,1,0:T(8,128)} %get-tuple-element.10), channel_id=1, source_target_pairs={{0,96},{32,128},{64,160},{96,192},{128,224},{160,0},{192,32},{224,... | collective-permute-start | bytes 2359304 | tf_op jit(solution)/shard_map/ppermute | solution.py:301
  29.7 2.2 %collective-permute-start.4 = (f32[6,128,256]{2,1,0:T(8,128)}, f32[6,128,256]{2,1,0:T(8,128)S(1)}, u32[]{:S(2)}, u32[]{:S(2)}) collective-permute-start(f32[6,128,256]{2,1,0:T(8,128)} %get-tuple-element.11), channel_id=1, source_target_pairs={{0,160},{32,192},{64,224},{96,0},{128,32},{160,64},{192,96},{224,1... | collective-permute-start | bytes 2359304 | tf_op jit(solution)/shard_map/ppermute | solution.py:301
  31.9 1.1 shard_map.19
  33.1 5.5 %collective-permute-start.2 = (f32[6,128,256]{2,1,0:T(8,128)S(1)}, f32[6,128,256]{2,1,0:T(8,128)}, u32[]{:S(2)}, u32[]{:S(2)}) collective-permute-start(f32[6,128,256]{2,1,0:T(8,128)S(1)} %shard_map.19), channel_id=1, source_target_pairs={{0,128},{32,160},{64,192},{96,224},{128,0},{160,32},{192,64},{224,... | collective-permute-start | bytes 2359304 | tf_op jit(solution)/shard_map/ppermute | solution.py:301
  38.6 0.6 collective-permute-start.5
  39.2 1.8 collective-permute-start.6
  41.0 72.6 %collective-permute-done.5.refs_3_ = f32[8,256]{1,0:T(8,128)S(1)} collective-permute-done((f32[8,256]{1,0:T(8,128)S(1)}, f32[8,256]{1,0:T(8,128)S(1)}, u32[]{:S(2)}, u32[]{:S(2)}) %collective-permute-start.5) | collective-permute-done | bytes 8224 | tf_op jit(solution)/shard_map/ppermute | solution.py:301
  113.6 9.7 %collective-permute-start.7 = (f32[8,256]{1,0:T(8,128)S(1)}, f32[8,256]{1,0:T(8,128)S(1)}, u32[]{:S(2)}, u32[]{:S(2)}) collective-permute-start(f32[8,256]{1,0:T(8,128)S(1)} %get-tuple-element.14), channel_id=1, source_target_pairs={{0,160},{32,192},{64,224},{96,0},{128,32},{160,64},{192,96},{224,1... | collective-permute-start | bytes 24584 | tf_op jit(solution)/shard_map/ppermute | solution.py:301
  123.3 1.4 collective-permute-done.7.refs_5_
  124.7 0.0 collective-permute-done.3.refs_1_
  124.7 0.5 copy-done.4
  125.3 0.3 copy-done
  125.6 0.4 copy-done.1
  125.9 4.5 %shard_map.22 = f32[8,3,6,32,128]{4,3,2,1,0:T(8,128)} custom-call(f32[6,128,256]{2,1,0:T(8,128)} %collective-permute-done.2.refs_0_, f32[6,128,256]{2,1,0:T(8,128)} %copy-done, f32[6,128,256]{2,1,0:T(8,128)} %copy-done.1, f32[8,256]{1,0:T(8,128)} %copy-done.2, f32[8,256]{1,0:T(8,128)} %copy-done.3, f32[8,256]{1,0:T(8,128)} %copy-done.4), custom_call_target="tpu_custom_call" | custom-call | tf_op jit(solution)/shard_map/pallas_call | solution.py:149
  130.4 4.8 %all-to-all-start.2 = ((f32[8,3,6,32,128]{4,3,2,1,0:T(8,128)}), f32[8,3,6,32,128]{4,3,2,1,0:T(8,128)}, u32[]{:S(2)}, u32[]{:S(2)}) async-start(f32[8,3,6,32,128]{4,3,2,1,0:T(8,128)} %shard_map.22), calls=%async_computation.2 | async-start | bytes 4718592 | tf_op jit(solution)/shard_map/all_to_all | solution.py:305
  135.2 3.7 %slice_bitcast_fusion = (f32[8,6,32,128]{3,2,1,0:T(8,128)}, f32[8,6,32,128]{3,2,1,0:T(8,128)}, f32[8,6,32,128]{3,2,1,0:T(8,128)}, f32[8,6,32,128]{3,2,1,0:T(8,128)}) fusion(f32[8,5,6,32,128]{4,3,2,1,0:T(8,128)} %all-to-all-done.1.piece_ref), kind=kLoop, calls=%fused_computation | loop fusion | bytes 6291456 | tf_op jit(solution)/shard_map/squeeze | solution.py:328
  138.9 2.2 %collective-permute-start.8 = (f32[8,6,32,128]{3,2,1,0:T(8,128)}, f32[8,6,32,128]{3,2,1,0:T(8,128)}, u32[]{:S(2)}, u32[]{:S(2)}) collective-permute-start(f32[8,6,32,128]{3,2,1,0:T(8,128)} %get-tuple-element.16), channel_id=1, source_target_pairs={{0,64},{32,96},{64,128},{96,160},{128,192},{160,224},{192,0},{224,... | collective-permute-start | bytes 2359304 | tf_op jit(solution)/shard_map/ppermute | solution.py:301
  141.1 2.0 collective-permute-start.9
  143.1 5.6 %collective-permute-start = (f32[8,6,32,128]{3,2,1,0:T(8,128)}, f32[8,6,32,128]{3,2,1,0:T(8,128)S(1)}, u32[]{:S(2)}, u32[]{:S(2)}) collective-permute-start(f32[8,6,32,128]{3,2,1,0:T(8,128)} %get-tuple-element.18), channel_id=1, source_target_pairs={{0,32},{32,64},{64,96},{96,128},{128,160},{160,192},{192,224},{224... | collective-permute-start | bytes 2359304 | tf_op jit(solution)/shard_map/ppermute | solution.py:301
  148.7 2.0 %shard_map.23.refs_2_ = f32[8,8,6,32,128]{4,3,2,1,0:T(8,128)} custom-call(f32[8,5,6,32,128]{4,3,2,1,0:T(8,128)} %all-to-all-done.1.piece_ref), custom_call_target="tpu_custom_call" | custom-call | tf_op jit(solution)/shard_map/pallas_call | solution.py:253
  150.7 12.5 %collective-permute-done.8.refs_0_ = f32[8,6,32,128]{3,2,1,0:T(8,128)} collective-permute-done((f32[8,6,32,128]{3,2,1,0:T(8,128)}, f32[8,6,32,128]{3,2,1,0:T(8,128)}, u32[]{:S(2)}, u32[]{:S(2)}) %collective-permute-start.8) | collective-permute-done | bytes 786464 | tf_op jit(solution)/shard_map/ppermute | solution.py:301
  163.2 0.6 collective-permute-done.9.refs_1_
  163.9 2.6 %shard_map.24.refs_0_ = f32[8,8,6,32,128]{4,3,2,1,0:T(8,128)} custom-call(f32[8,6,32,128]{3,2,1,0:T(8,128)} %collective-permute-done.8.refs_0_, f32[8,6,32,128]{3,2,1,0:T(8,128)} %collective-permute-done.9.refs_1_, f32[8,8,6,32,128]{4,3,2,1,0:T(8,128)} %shard_map.23.refs_2_), custom_call_target="tpu_custom_call", output_to_operand_aliasing={{}: (2, {})} | custom-call | tf_op jit(solution)/shard_map/pallas_call | solution.py:289
  166.4 2.6 %shard_map.25.refs_2_ = f32[8,8,6,32,128]{4,3,2,1,0:T(8,128)} custom-call(f32[8,3,6,32,128]{4,3,2,1,0:T(8,128)} %all-to-all-done.2.piece_ref, f32[8,8,6,32,128]{4,3,2,1,0:T(8,128)} %shard_map.24.refs_0_), custom_call_target="tpu_custom_call", output_to_operand_aliasing={{}: (1, {})} | custom-call | tf_op jit(solution)/shard_map/pallas_call | solution.py:253
  169.0 26.9 %collective-permute-done.refs_0_ = f32[8,6,32,128]{3,2,1,0:T(8,128)S(1)} collective-permute-done((f32[8,6,32,128]{3,2,1,0:T(8,128)}, f32[8,6,32,128]{3,2,1,0:T(8,128)S(1)}, u32[]{:S(2)}, u32[]{:S(2)}) %collective-permute-start) | collective-permute-done | bytes 786464 | tf_op jit(solution)/shard_map/ppermute | solution.py:301
  195.9 0.7 collective-permute-done.1.refs_1_
  196.6 1.2 shard_map.26
  (14 shorter events, 0.1 us)
Async XLA Ops:
  17.7 112.6 %all-to-all-start.1 = ((f32[8,5,6,32,128]{4,3,2,1,0:T(8,128)}), f32[8,5,6,32,128]{4,3,2,1,0:T(8,128)}, u32[]{:S(2)}, u32[]{:S(2)}) async-start(f32[8,5,6,32,128]{4,3,2,1,0:T(8,128)} %shard_map.18), calls=%async_computation.1 | async-start | bytes 7864320 | tf_op jit(solution)/shard_map/all_to_all | solution.py:305
  25.0 99.7 %collective-permute-start.3 = (f32[6,128,256]{2,1,0:T(8,128)}, f32[6,128,256]{2,1,0:T(8,128)S(1)}, u32[]{:S(2)}, u32[]{:S(2)}) collective-permute-start(f32[6,128,256]{2,1,0:T(8,128)} %get-tuple-element.10), channel_id=1, source_target_pairs={{0,96},{32,128},{64,160},{96,192},{128,224},{160,0},{192,32},{224,... | collective-permute-start | bytes 2359304 | tf_op jit(solution)/shard_map/ppermute | solution.py:301
  29.7 95.0 %collective-permute-start.4 = (f32[6,128,256]{2,1,0:T(8,128)}, f32[6,128,256]{2,1,0:T(8,128)S(1)}, u32[]{:S(2)}, u32[]{:S(2)}) collective-permute-start(f32[6,128,256]{2,1,0:T(8,128)} %get-tuple-element.11), channel_id=1, source_target_pairs={{0,160},{32,192},{64,224},{96,0},{128,32},{160,64},{192,96},{224,1... | collective-permute-start | bytes 2359304 | tf_op jit(solution)/shard_map/ppermute | solution.py:301
  33.1 91.6 %collective-permute-start.2 = (f32[6,128,256]{2,1,0:T(8,128)S(1)}, f32[6,128,256]{2,1,0:T(8,128)}, u32[]{:S(2)}, u32[]{:S(2)}) collective-permute-start(f32[6,128,256]{2,1,0:T(8,128)S(1)} %shard_map.19), channel_id=1, source_target_pairs={{0,128},{32,160},{64,192},{96,224},{128,0},{160,32},{192,64},{224,... | collective-permute-start | bytes 2359304 | tf_op jit(solution)/shard_map/ppermute | solution.py:301
  38.6 75.0 %collective-permute-start.5 = (f32[8,256]{1,0:T(8,128)S(1)}, f32[8,256]{1,0:T(8,128)S(1)}, u32[]{:S(2)}, u32[]{:S(2)}) collective-permute-start(f32[8,256]{1,0:T(8,128)S(1)} %get-tuple-element.12), channel_id=1, source_target_pairs={{0,128},{32,160},{64,192},{96,224},{128,0},{160,32},{192,64},{224,... | collective-permute-start | bytes 24584 | tf_op jit(solution)/shard_map/ppermute | solution.py:301
  39.2 84.1 %collective-permute-start.6 = (f32[8,256]{1,0:T(8,128)S(1)}, f32[8,256]{1,0:T(8,128)S(1)}, u32[]{:S(2)}, u32[]{:S(2)}) collective-permute-start(f32[8,256]{1,0:T(8,128)S(1)} %get-tuple-element.13), channel_id=1, source_target_pairs={{0,96},{32,128},{64,160},{96,192},{128,224},{160,0},{192,32},{224,... | collective-permute-start | bytes 24584 | tf_op jit(solution)/shard_map/ppermute | solution.py:301
  113.6 11.1 %copy-start.2 = (f32[8,256]{1,0:T(8,128)}, f32[8,256]{1,0:T(8,128)S(1)}, u32[]{:S(2)}) copy-start(f32[8,256]{1,0:T(8,128)S(1)} %collective-permute-done.5.refs_3_) | copy-start | bytes 24580
  113.6 11.0 %collective-permute-start.7 = (f32[8,256]{1,0:T(8,128)S(1)}, f32[8,256]{1,0:T(8,128)S(1)}, u32[]{:S(2)}, u32[]{:S(2)}) collective-permute-start(f32[8,256]{1,0:T(8,128)S(1)} %get-tuple-element.14), channel_id=1, source_target_pairs={{0,160},{32,192},{64,224},{96,0},{128,32},{160,64},{192,96},{224,1... | collective-permute-start | bytes 24584 | tf_op jit(solution)/shard_map/ppermute | solution.py:301
  123.3 1.4 copy-start.3
  124.7 0.6 copy-start.4
  124.7 0.9 copy-start
  124.7 1.2 copy-start.1
  130.4 36.0 %all-to-all-start.2 = ((f32[8,3,6,32,128]{4,3,2,1,0:T(8,128)}), f32[8,3,6,32,128]{4,3,2,1,0:T(8,128)}, u32[]{:S(2)}, u32[]{:S(2)}) async-start(f32[8,3,6,32,128]{4,3,2,1,0:T(8,128)} %shard_map.22), calls=%async_computation.2 | async-start | bytes 4718592 | tf_op jit(solution)/shard_map/all_to_all | solution.py:305
  138.9 24.4 %collective-permute-start.8 = (f32[8,6,32,128]{3,2,1,0:T(8,128)}, f32[8,6,32,128]{3,2,1,0:T(8,128)}, u32[]{:S(2)}, u32[]{:S(2)}) collective-permute-start(f32[8,6,32,128]{3,2,1,0:T(8,128)} %get-tuple-element.16), channel_id=1, source_target_pairs={{0,64},{32,96},{64,128},{96,160},{128,192},{160,224},{192,0},{224,... | collective-permute-start | bytes 2359304 | tf_op jit(solution)/shard_map/ppermute | solution.py:301
  141.1 22.7 %collective-permute-start.9 = (f32[8,6,32,128]{3,2,1,0:T(8,128)}, f32[8,6,32,128]{3,2,1,0:T(8,128)}, u32[]{:S(2)}, u32[]{:S(2)}) collective-permute-start(f32[8,6,32,128]{3,2,1,0:T(8,128)} %get-tuple-element.15), channel_id=1, source_target_pairs={{0,192},{32,224},{64,0},{96,32},{128,64},{160,96},{192,128},{224,1... | collective-permute-start | bytes 2359304 | tf_op jit(solution)/shard_map/ppermute | solution.py:301
  143.1 52.8 %collective-permute-start = (f32[8,6,32,128]{3,2,1,0:T(8,128)}, f32[8,6,32,128]{3,2,1,0:T(8,128)S(1)}, u32[]{:S(2)}, u32[]{:S(2)}) collective-permute-start(f32[8,6,32,128]{3,2,1,0:T(8,128)} %get-tuple-element.18), channel_id=1, source_target_pairs={{0,32},{32,64},{64,96},{96,128},{128,160},{160,192},{192,224},{224... | collective-permute-start | bytes 2359304 | tf_op jit(solution)/shard_map/ppermute | solution.py:301
  148.7 47.9 %collective-permute-start.1 = (f32[8,6,32,128]{3,2,1,0:T(8,128)}, f32[8,6,32,128]{3,2,1,0:T(8,128)S(1)}, u32[]{:S(2)}, u32[]{:S(2)}) collective-permute-start(f32[8,6,32,128]{3,2,1,0:T(8,128)} %get-tuple-element.17), channel_id=1, source_target_pairs={{0,224},{32,0},{64,32},{96,64},{128,96},{160,128},{192,160},{224,1... | collective-permute-start | bytes 2359304 | tf_op jit(solution)/shard_map/ppermute | solution.py:301
where the time goes:
time: 200 us; the launch traced here: 198 us
  waiting for transfers between devices  115 us (58%)
  starting transfers between devices  44.1 us (22%)
  Pallas kernels  24.2 us (12%)
  blocking collectives  9.85 us (5%)
  local copies, waits for them, and re-layouts  4.9 us (2%)
    ppermute x10, waiting for transfers between devices, shifted(): lax.ppermute(block, 'space_0', [(i, (i + step) % ring) for i in range(rin...  115 us
    ppermute x10, starting transfers between devices, shifted(): lax.ppermute(block, 'space_0', [(i, (i + step) % ring) for i in range(rin...  34.3 us
    all_to_all x1, blocking collectives, exchanged(): return lax.all_to_all(value, axes, split_axis=0, concat_axis=0, tiled=True)  9.85 us
    all_to_all x2, starting transfers between devices, exchanged(): return lax.all_to_all(value, axes, split_axis=0, concat_axis=0, tiled=True)  9.75 us
    pallas_call x2, Pallas kernels, running_call(): pl.pallas_call(body, compiler_params=params, in_specs=specs, out_specs=IN...  9.37 us
    pallas_call x2, Pallas kernels, place(): pl.pallas_call(functools.partial(place_kernel, steps=steps), compiler_par...  4.61 us
  transfers between devices with their start and end apart: 12, of which 6 were waited for; matrix products, arithmetic and copies ran while one was open for 2% of the time, Pallas kernels for 8%

commit v1 on v0

--- a/solution.py
+++ b/solution.py
@@ -9,10 +9,9 @@
 from jax.sharding import PartitionSpec as P
 
 PLANE = ("space_1", "space_2")
-RING_FIRST = (4, 3, -3)
-PLANE_FIRST = (0, 1, -1, 2, -2)
+RING_FIRST = (4, -3, 3)
+PLANE_FIRST = (0, -1, 1, -2, 2)
 PARTS = 3
-PIECES = 4
 
 IN_VMEM = pl.BlockSpec(memory_space=pltpu.VMEM)
 IN_HBM = pl.BlockSpec(memory_space=pl.ANY)
@@ -269,13 +268,12 @@
     n = len(steps)
     block_refs, whole_ref, sems = refs[:n], refs[n + 1], refs[n + 2]
     ring = whole_ref.shape[0]
-    part = block_refs[0].shape[0] // PIECES
-    copies = []
-    for k, step in enumerate(steps):
-        for p in range(PIECES):
-            source = block_refs[k].at[pl.ds(p * part, part)]
-            target = whole_ref.at[ring_place(-step, ring), pl.ds(p * part, part)]
-            copies.append(pltpu.make_async_copy(source, target, sems.at[k, p]))
+    copies = [
+        pltpu.make_async_copy(
+            block_refs[k], whole_ref.at[ring_place(-step, ring)], sems.at[k]
+        )
+        for k, step in enumerate(steps)
+    ]
     for copy in copies:
         copy.start()
     for copy in copies:
@@ -292,7 +290,7 @@
         in_specs=[IN_VMEM] * n + [IN_HBM],
         out_specs=IN_HBM,
         out_shape=jax.ShapeDtypeStruct(whole.shape, jnp.float32),
-        scratch_shapes=[pltpu.SemaphoreType.DMA((n, PIECES))],
+        scratch_shapes=[pltpu.SemaphoreType.DMA((n,))],
         input_output_aliases={n: 0},
     )(*blocks, whole)
 

time: 200 us -> 200 us (level)
  waiting for transfers between devices: 115 us -> 120 us
  starting transfers between devices: 44.1 us -> 40.1 us
    ppermute x10, waiting for transfers between devices: 115 us -> 120 us  [shifted(): lax.ppermute(block, 'space_0', [(i, (i + step) % ring) for i in range(rin...]
    ppermute x10, starting transfers between devices: 34.3 us -> 30.3 us  [shifted(): lax.ppermute(block, 'space_0', [(i, (i + step) % ring) for i in range(rin...]
  transfers between devices with their start and end apart: 12 -> 12, of which waited for: 6 -> 7; matrix products, arithmetic and copies ran while one was open for 2% -> 2% of each run, Pallas kernels for 8% -> 8%
where the time goes in v1:
time: 200 us; the launch traced here: 199 us
  waiting for transfers between devices  120 us (60%)
  starting transfers between devices  40.1 us (20%)
  Pallas kernels  24.1 us (12%)
  blocking collectives  9.85 us (5%)
  local copies, waits for them, and re-layouts  4.9 us (2%)
    ppermute x10, waiting for transfers between devices, shifted(): lax.ppermute(block, 'space_0', [(i, (i + step) % ring) for i in range(rin...  120 us
    ppermute x10, starting transfers between devices, shifted(): lax.ppermute(block, 'space_0', [(i, (i + step) % ring) for i in range(rin...  30.3 us
    all_to_all x1, blocking collectives, exchanged(): return lax.all_to_all(value, axes, split_axis=0, concat_axis=0, tiled=True)  9.85 us
    all_to_all x2, starting transfers between devices, exchanged(): return lax.all_to_all(value, axes, split_axis=0, concat_axis=0, tiled=True)  9.74 us
    pallas_call x2, Pallas kernels, running_call(): pl.pallas_call(body, compiler_params=params, in_specs=specs, out_specs=IN...  9.37 us
    pallas_call x2, Pallas kernels, place(): pl.pallas_call(functools.partial(place_kernel, steps=steps), compiler_par...  4.61 us
  transfers between devices with their start and end apart: 12, of which 7 were waited for; matrix products, arithmetic and copies ran while one was open for 2% of the time, Pallas kernels for 8%

profile of v1, /device:TPU:10, one launch (start us, length us, event | category | flops | bytes accessed | tf_op | source)
XLA Modules:
  0.0 198.6 jit_solution(6110782245894531341)
XLA Ops:
  0.0 3.0 %shard_map.17 = f32[4,6,2048]{2,1,0:T(8,128)S(1)} custom-call(f32[6,128,2048]{2,1,0:T(8,128)} %bitcast.18), custom_call_target="tpu_custom_call" | custom-call | tf_op jit(solution)/shard_map/pallas_call | solution.py:201
  3.0 9.8 %all_to_all.15.theirs_ref = f32[4,6,2048]{2,1,0:T(8,128)S(1)} all-to-all(f32[4,6,2048]{2,1,0:T(8,128)S(1)} %shard_map.17), channel_id=1, replica_groups=mesh['space_0'=8,'space_1'=4,'space_2'=2,'tm'=4] {'tm'}, dimensions={0} | all-to-all | bytes 393216 | tf_op jit(solution)/shard_map/all_to_all | solution.py:303
  12.8 4.9 %shard_map.18 = f32[8,5,6,32,128]{4,3,2,1,0:T(8,128)} custom-call(f32[6,128,2048]{2,1,0:T(8,128)} %bitcast.19, f32[4,6,2048]{2,1,0:T(8,128)S(1)} %all_to_all.15.theirs_ref), custom_call_target="tpu_custom_call" | custom-call | tf_op jit(solution)/shard_map/pallas_call | solution.py:148
  17.7 4.9 %all-to-all-start.1 = ((f32[8,5,6,32,128]{4,3,2,1,0:T(8,128)}), f32[8,5,6,32,128]{4,3,2,1,0:T(8,128)}, u32[]{:S(2)}, u32[]{:S(2)}) async-start(f32[8,5,6,32,128]{4,3,2,1,0:T(8,128)} %shard_map.18), calls=%async_computation.1 | async-start | bytes 7864320 | tf_op jit(solution)/shard_map/all_to_all | solution.py:303
  22.7 2.3 %shard_map.20 = (f32[6,128,256]{2,1,0:T(8,128)}, f32[6,128,256]{2,1,0:T(8,128)}) custom-call(f32[6,128,2048]{2,1,0:T(8,128)} %bitcast.20), custom_call_target="tpu_custom_call" | custom-call | tf_op jit(solution)/shard_map/pallas_call | solution.py:106
  25.0 6.8 %collective-permute-start.3 = (f32[6,128,256]{2,1,0:T(8,128)}, f32[6,128,256]{2,1,0:T(8,128)S(1)}, u32[]{:S(2)}, u32[]{:S(2)}) collective-permute-start(f32[6,128,256]{2,1,0:T(8,128)} %get-tuple-element.10), channel_id=1, source_target_pairs={{0,160},{32,192},{64,224},{96,0},{128,32},{160,64},{192,96},{224,1... | collective-permute-start | bytes 2359304 | tf_op jit(solution)/shard_map/ppermute | solution.py:299
  31.8 1.1 shard_map.19
  33.0 4.3 %collective-permute-start.2 = (f32[6,128,256]{2,1,0:T(8,128)S(1)}, f32[6,128,256]{2,1,0:T(8,128)}, u32[]{:S(2)}, u32[]{:S(2)}) collective-permute-start(f32[6,128,256]{2,1,0:T(8,128)S(1)} %shard_map.19), channel_id=1, source_target_pairs={{0,128},{32,160},{64,192},{96,224},{128,0},{160,32},{192,64},{224,... | collective-permute-start | bytes 2359304 | tf_op jit(solution)/shard_map/ppermute | solution.py:299
  37.4 1.8 collective-permute-start.5
  39.1 5.0 %collective-permute-start.6 = (f32[8,256]{1,0:T(8,128)S(1)}, f32[8,256]{1,0:T(8,128)S(1)}, u32[]{:S(2)}, u32[]{:S(2)}) collective-permute-start(f32[8,256]{1,0:T(8,128)S(1)} %get-tuple-element.13), channel_id=1, source_target_pairs={{0,160},{32,192},{64,224},{96,0},{128,32},{160,64},{192,96},{224,1... | collective-permute-start | bytes 24584 | tf_op jit(solution)/shard_map/ppermute | solution.py:299
  44.2 64.1 %collective-permute-done.5.refs_3_ = f32[8,256]{1,0:T(8,128)S(1)} collective-permute-done((f32[8,256]{1,0:T(8,128)S(1)}, f32[8,256]{1,0:T(8,128)S(1)}, u32[]{:S(2)}, u32[]{:S(2)}) %collective-permute-start.5) | collective-permute-done | bytes 8224 | tf_op jit(solution)/shard_map/ppermute | solution.py:299
  108.2 2.6 %collective-permute-start.7 = (f32[8,256]{1,0:T(8,128)S(1)}, f32[8,256]{1,0:T(8,128)S(1)}, u32[]{:S(2)}, u32[]{:S(2)}) collective-permute-start(f32[8,256]{1,0:T(8,128)S(1)} %get-tuple-element.14), channel_id=1, source_target_pairs={{0,96},{32,128},{64,160},{96,192},{128,224},{160,0},{192,32},{224,... | collective-permute-start | bytes 24584 | tf_op jit(solution)/shard_map/ppermute | solution.py:299
  110.8 6.9 %collective-permute-done.6.refs_4_ = f32[8,256]{1,0:T(8,128)S(1)} collective-permute-done((f32[8,256]{1,0:T(8,128)S(1)}, f32[8,256]{1,0:T(8,128)S(1)}, u32[]{:S(2)}, u32[]{:S(2)}) %collective-permute-start.6) | collective-permute-done | bytes 8224 | tf_op jit(solution)/shard_map/ppermute | solution.py:299
  117.8 5.1 %collective-permute-done.7.refs_5_ = f32[8,256]{1,0:T(8,128)S(1)} collective-permute-done((f32[8,256]{1,0:T(8,128)S(1)}, f32[8,256]{1,0:T(8,128)S(1)}, u32[]{:S(2)}, u32[]{:S(2)}) %collective-permute-start.7) | collective-permute-done | bytes 8224 | tf_op jit(solution)/shard_map/ppermute | solution.py:299
  122.9 0.5 copy-done.4
  123.4 0.3 copy-done
  123.7 0.4 copy-done.1
  124.1 4.5 %shard_map.22 = f32[8,3,6,32,128]{4,3,2,1,0:T(8,128)} custom-call(f32[6,128,256]{2,1,0:T(8,128)} %collective-permute-done.2.refs_0_, f32[6,128,256]{2,1,0:T(8,128)} %copy-done, f32[6,128,256]{2,1,0:T(8,128)} %copy-done.1, f32[8,256]{1,0:T(8,128)} %copy-done.2, f32[8,256]{1,0:T(8,128)} %copy-done.3, f32[8,256]{1,0:T(8,128)} %copy-done.4), custom_call_target="tpu_custom_call" | custom-call | tf_op jit(solution)/shard_map/pallas_call | solution.py:148
  128.5 4.8 %all-to-all-start.2 = ((f32[8,3,6,32,128]{4,3,2,1,0:T(8,128)}), f32[8,3,6,32,128]{4,3,2,1,0:T(8,128)}, u32[]{:S(2)}, u32[]{:S(2)}) async-start(f32[8,3,6,32,128]{4,3,2,1,0:T(8,128)} %shard_map.22), calls=%async_computation.2 | async-start | bytes 4718592 | tf_op jit(solution)/shard_map/all_to_all | solution.py:303
  133.4 3.7 %slice_bitcast_fusion = (f32[8,6,32,128]{3,2,1,0:T(8,128)}, f32[8,6,32,128]{3,2,1,0:T(8,128)}, f32[8,6,32,128]{3,2,1,0:T(8,128)}, f32[8,6,32,128]{3,2,1,0:T(8,128)}) fusion(f32[8,5,6,32,128]{4,3,2,1,0:T(8,128)} %all-to-all-done.1.piece_ref), kind=kLoop, calls=%fused_computation | loop fusion | bytes 6291456 | tf_op jit(solution)/shard_map/squeeze | solution.py:326
  137.1 6.5 %collective-permute-start.8 = (f32[8,6,32,128]{3,2,1,0:T(8,128)}, f32[8,6,32,128]{3,2,1,0:T(8,128)}, u32[]{:S(2)}, u32[]{:S(2)}) collective-permute-start(f32[8,6,32,128]{3,2,1,0:T(8,128)} %get-tuple-element.16), channel_id=1, source_target_pairs={{0,192},{32,224},{64,0},{96,32},{128,64},{160,96},{192,128},{224,1... | collective-permute-start | bytes 2359304 | tf_op jit(solution)/shard_map/ppermute | solution.py:299
  143.5 1.3 collective-permute-start.9
  144.8 1.5 collective-permute-start
  146.3 0.5 collective-permute-start.1
  146.8 2.0 %shard_map.23.refs_2_ = f32[8,8,6,32,128]{4,3,2,1,0:T(8,128)} custom-call(f32[8,5,6,32,128]{4,3,2,1,0:T(8,128)} %all-to-all-done.1.piece_ref), custom_call_target="tpu_custom_call" | custom-call | tf_op jit(solution)/shard_map/pallas_call | solution.py:252
  148.9 29.0 %collective-permute-done.8.refs_0_ = f32[8,6,32,128]{3,2,1,0:T(8,128)} collective-permute-done((f32[8,6,32,128]{3,2,1,0:T(8,128)}, f32[8,6,32,128]{3,2,1,0:T(8,128)}, u32[]{:S(2)}, u32[]{:S(2)}) %collective-permute-start.8) | collective-permute-done | bytes 786464 | tf_op jit(solution)/shard_map/ppermute | solution.py:299
  177.8 2.9 %collective-permute-done.9.refs_1_ = f32[8,6,32,128]{3,2,1,0:T(8,128)} collective-permute-done((f32[8,6,32,128]{3,2,1,0:T(8,128)}, f32[8,6,32,128]{3,2,1,0:T(8,128)}, u32[]{:S(2)}, u32[]{:S(2)}) %collective-permute-start.9) | collective-permute-done | bytes 786464 | tf_op jit(solution)/shard_map/ppermute | solution.py:299
  180.7 2.5 %shard_map.24.refs_0_ = f32[8,8,6,32,128]{4,3,2,1,0:T(8,128)} custom-call(f32[8,6,32,128]{3,2,1,0:T(8,128)} %collective-permute-done.8.refs_0_, f32[8,6,32,128]{3,2,1,0:T(8,128)} %collective-permute-done.9.refs_1_, f32[8,8,6,32,128]{4,3,2,1,0:T(8,128)} %shard_map.23.refs_2_), custom_call_target="tpu_custom_call", output_to_operand_aliasing={{}: (2, {})} | custom-call | tf_op jit(solution)/shard_map/pallas_call | solution.py:287
  183.2 2.6 %shard_map.25.refs_2_ = f32[8,8,6,32,128]{4,3,2,1,0:T(8,128)} custom-call(f32[8,3,6,32,128]{4,3,2,1,0:T(8,128)} %all-to-all-done.2.piece_ref, f32[8,8,6,32,128]{4,3,2,1,0:T(8,128)} %shard_map.24.refs_0_), custom_call_target="tpu_custom_call", output_to_operand_aliasing={{}: (1, {})} | custom-call | tf_op jit(solution)/shard_map/pallas_call | solution.py:252
  185.8 9.3 %collective-permute-done.refs_0_ = f32[8,6,32,128]{3,2,1,0:T(8,128)S(1)} collective-permute-done((f32[8,6,32,128]{3,2,1,0:T(8,128)}, f32[8,6,32,128]{3,2,1,0:T(8,128)S(1)}, u32[]{:S(2)}, u32[]{:S(2)}) %collective-permute-start) | collective-permute-done | bytes 786464 | tf_op jit(solution)/shard_map/ppermute | solution.py:299
  195.1 2.4 %collective-permute-done.1.refs_1_ = f32[8,6,32,128]{3,2,1,0:T(8,128)S(1)} collective-permute-done((f32[8,6,32,128]{3,2,1,0:T(8,128)}, f32[8,6,32,128]{3,2,1,0:T(8,128)S(1)}, u32[]{:S(2)}, u32[]{:S(2)}) %collective-permute-start.1) | collective-permute-done | bytes 786464 | tf_op jit(solution)/shard_map/ppermute | solution.py:299
  197.5 1.2 shard_map.26
  (14 shorter events, 0.1 us)
Async XLA Ops:
  17.7 110.8 %all-to-all-start.1 = ((f32[8,5,6,32,128]{4,3,2,1,0:T(8,128)}), f32[8,5,6,32,128]{4,3,2,1,0:T(8,128)}, u32[]{:S(2)}, u32[]{:S(2)}) async-start(f32[8,5,6,32,128]{4,3,2,1,0:T(8,128)} %shard_map.18), calls=%async_computation.1 | async-start | bytes 7864320 | tf_op jit(solution)/shard_map/all_to_all | solution.py:303
  25.0 97.8 %collective-permute-start.3 = (f32[6,128,256]{2,1,0:T(8,128)}, f32[6,128,256]{2,1,0:T(8,128)S(1)}, u32[]{:S(2)}, u32[]{:S(2)}) collective-permute-start(f32[6,128,256]{2,1,0:T(8,128)} %get-tuple-element.10), channel_id=1, source_target_pairs={{0,160},{32,192},{64,224},{96,0},{128,32},{160,64},{192,96},{224,1... | collective-permute-start | bytes 2359304 | tf_op jit(solution)/shard_map/ppermute | solution.py:299
  31.8 91.0 %collective-permute-start.4 = (f32[6,128,256]{2,1,0:T(8,128)}, f32[6,128,256]{2,1,0:T(8,128)S(1)}, u32[]{:S(2)}, u32[]{:S(2)}) collective-permute-start(f32[6,128,256]{2,1,0:T(8,128)} %get-tuple-element.11), channel_id=1, source_target_pairs={{0,96},{32,128},{64,160},{96,192},{128,224},{160,0},{192,32},{224,... | collective-permute-start | bytes 2359304 | tf_op jit(solution)/shard_map/ppermute | solution.py:299
  33.0 89.9 %collective-permute-start.2 = (f32[6,128,256]{2,1,0:T(8,128)S(1)}, f32[6,128,256]{2,1,0:T(8,128)}, u32[]{:S(2)}, u32[]{:S(2)}) collective-permute-start(f32[6,128,256]{2,1,0:T(8,128)S(1)} %shard_map.19), channel_id=1, source_target_pairs={{0,128},{32,160},{64,192},{96,224},{128,0},{160,32},{192,64},{224,... | collective-permute-start | bytes 2359304 | tf_op jit(solution)/shard_map/ppermute | solution.py:299
  37.4 70.8 %collective-permute-start.5 = (f32[8,256]{1,0:T(8,128)S(1)}, f32[8,256]{1,0:T(8,128)S(1)}, u32[]{:S(2)}, u32[]{:S(2)}) collective-permute-start(f32[8,256]{1,0:T(8,128)S(1)} %get-tuple-element.12), channel_id=1, source_target_pairs={{0,128},{32,160},{64,192},{96,224},{128,0},{160,32},{192,64},{224,... | collective-permute-start | bytes 24584 | tf_op jit(solution)/shard_map/ppermute | solution.py:299
  39.1 78.6 %collective-permute-start.6 = (f32[8,256]{1,0:T(8,128)S(1)}, f32[8,256]{1,0:T(8,128)S(1)}, u32[]{:S(2)}, u32[]{:S(2)}) collective-permute-start(f32[8,256]{1,0:T(8,128)S(1)} %get-tuple-element.13), channel_id=1, source_target_pairs={{0,160},{32,192},{64,224},{96,0},{128,32},{160,64},{192,96},{224,1... | collective-permute-start | bytes 24584 | tf_op jit(solution)/shard_map/ppermute | solution.py:299
  108.2 14.6 %copy-start.2 = (f32[8,256]{1,0:T(8,128)}, f32[8,256]{1,0:T(8,128)S(1)}, u32[]{:S(2)}) copy-start(f32[8,256]{1,0:T(8,128)S(1)} %collective-permute-done.5.refs_3_) | copy-start | bytes 24580
  108.2 14.6 %collective-permute-start.7 = (f32[8,256]{1,0:T(8,128)S(1)}, f32[8,256]{1,0:T(8,128)S(1)}, u32[]{:S(2)}, u32[]{:S(2)}) collective-permute-start(f32[8,256]{1,0:T(8,128)S(1)} %get-tuple-element.14), channel_id=1, source_target_pairs={{0,96},{32,128},{64,160},{96,192},{128,224},{160,0},{192,32},{224,... | collective-permute-start | bytes 24584 | tf_op jit(solution)/shard_map/ppermute | solution.py:299
  117.8 5.1 %copy-start.3 = (f32[8,256]{1,0:T(8,128)}, f32[8,256]{1,0:T(8,128)S(1)}, u32[]{:S(2)}) copy-start(f32[8,256]{1,0:T(8,128)S(1)} %collective-permute-done.6.refs_4_) | copy-start | bytes 24580
  122.8 0.6 copy-start.4
  122.8 0.9 copy-start
  122.8 1.2 copy-start.1
  128.5 54.7 %all-to-all-start.2 = ((f32[8,3,6,32,128]{4,3,2,1,0:T(8,128)}), f32[8,3,6,32,128]{4,3,2,1,0:T(8,128)}, u32[]{:S(2)}, u32[]{:S(2)}) async-start(f32[8,3,6,32,128]{4,3,2,1,0:T(8,128)} %shard_map.22), calls=%async_computation.2 | async-start | bytes 4718592 | tf_op jit(solution)/shard_map/all_to_all | solution.py:303
  137.1 40.8 %collective-permute-start.8 = (f32[8,6,32,128]{3,2,1,0:T(8,128)}, f32[8,6,32,128]{3,2,1,0:T(8,128)}, u32[]{:S(2)}, u32[]{:S(2)}) collective-permute-start(f32[8,6,32,128]{3,2,1,0:T(8,128)} %get-tuple-element.16), channel_id=1, source_target_pairs={{0,192},{32,224},{64,0},{96,32},{128,64},{160,96},{192,128},{224,1... | collective-permute-start | bytes 2359304 | tf_op jit(solution)/shard_map/ppermute | solution.py:299
  143.5 37.2 %collective-permute-start.9 = (f32[8,6,32,128]{3,2,1,0:T(8,128)}, f32[8,6,32,128]{3,2,1,0:T(8,128)}, u32[]{:S(2)}, u32[]{:S(2)}) collective-permute-start(f32[8,6,32,128]{3,2,1,0:T(8,128)} %get-tuple-element.15), channel_id=1, source_target_pairs={{0,64},{32,96},{64,128},{96,160},{128,192},{160,224},{192,0},{224,... | collective-permute-start | bytes 2359304 | tf_op jit(solution)/shard_map/ppermute | solution.py:299
  144.8 50.3 %collective-permute-start = (f32[8,6,32,128]{3,2,1,0:T(8,128)}, f32[8,6,32,128]{3,2,1,0:T(8,128)S(1)}, u32[]{:S(2)}, u32[]{:S(2)}) collective-permute-start(f32[8,6,32,128]{3,2,1,0:T(8,128)} %get-tuple-element.18), channel_id=1, source_target_pairs={{0,224},{32,0},{64,32},{96,64},{128,96},{160,128},{192,160},{224,1... | collective-permute-start | bytes 2359304 | tf_op jit(solution)/shard_map/ppermute | solution.py:299
  146.3 51.2 %collective-permute-start.1 = (f32[8,6,32,128]{3,2,1,0:T(8,128)}, f32[8,6,32,128]{3,2,1,0:T(8,128)S(1)}, u32[]{:S(2)}, u32[]{:S(2)}) collective-permute-start(f32[8,6,32,128]{3,2,1,0:T(8,128)} %get-tuple-element.17), channel_id=1, source_target_pairs={{0,32},{32,64},{64,96},{96,128},{128,160},{160,192},{192,224},{224... | collective-permute-start | bytes 2359304 | tf_op jit(solution)/shard_map/ppermute | solution.py:299
